TPU v7x, 256 devices: a whole 4x4x8 slice. The times are simulated.
256 devices in a mesh: dp: 8 (over z), expert: 32 (over x, y, core).
Axes of the slice: x: 4, y: 4, z: 8, core: 2. Of those that a mesh axis runs over, the one named last changes fastest.
Arguments:
- tokens: bfloat16 [65536, 2048], P(('dp', 'expert')), may hold values from -6 to 6
- expert_ranks: int32 [32, 65536], P(None, ('dp', 'expert')), may hold values from 0 to 65535, as said below
- capacity: int32 [32], replicated, may hold values from 512 to 1024, as said below
- weight_in: bfloat16 [32, 2048, 8192], P('expert', None, 'dp'), may hold values from -0.125 to 0.125
- weight_out: bfloat16 [32, 8192, 2048], P('expert', 'dp'), may hold values from -0.0625 to 0.0625
- gate_weights: float32 [32, 1024], P('expert', 'dp'), may hold values from 0.05 to 1
Outputs:
- combined: bfloat16 [65536, 2048], P(('dp', 'expert'))
Inputs may be any that keep to these rules, and one draw needn't show every extreme that they name: `expert_ranks`: for each expert the ranks are a permutation of 0 to 65535. Of the 256 tokens of one device, at most 8 have rank under 1024 for one expert; for an expert of capacity 1024, some devices have exactly 8. At least one expert has capacity 1024.
All inputs are finite; a program needn't handle non-finite values.
Results may differ from a plain program's by a relative error of at most 0.0053.
Values may be sent and summed in bfloat16 or wider, within the bound.
No kernel may reach another device: no remote copies, remote signals or barrier semaphores. Data moves between devices by JAX's collectives and lax.ppermute only.
A program may use at most 64 MiB of HBM per device.

v0:
```python
import jax
import jax.numpy as jnp
from jax import lax
from jax.sharding import Mesh
from jax.sharding import PartitionSpec as P

MOST = 8
LANES = 128
EXPERT = ("expert_0", "expert_1", "expert_2")
DP_EXPERT = ("dp", "expert_0", "expert_1", "expert_2")


def exclusive(values):
    return jnp.cumsum(values) - values


def on_device(tokens, expert_ranks, capacity, weight_in, weight_out, gate_weights):
    dp_count = lax.axis_size("dp")
    expert_count = lax.axis_size(EXPERT)
    token_count, width = tokens.shape
    slots_dp = gate_weights.shape[1]
    rows_all = expert_count * MOST
    own_dp = lax.axis_index("dp")
    own_expert = lax.axis_index(EXPERT)
    chosen = expert_ranks < capacity[:, None]
    chosen_int = chosen.astype(jnp.int32)
    counts = jnp.sum(chosen_int, axis=1)
    before = jnp.cumsum(chosen_int, axis=1) - chosen_int
    places = lax.broadcasted_iota(jnp.int32, (expert_count, MOST, token_count), 1)
    pack_table = jnp.logical_and(chosen[:, None, :], before[:, None, :] == places)
    pack_table = pack_table.astype(jnp.bfloat16).reshape(rows_all, token_count)
    packed = jnp.dot(pack_table, tokens, preferred_element_type=jnp.float32).astype(jnp.bfloat16)
    arrived_rows = lax.all_to_all(
        packed.reshape(expert_count, MOST, width), EXPERT, split_axis=0, concat_axis=0, tiled=True
    ).reshape(rows_all, width)
    device_ids = lax.broadcasted_iota(jnp.int32, (expert_count, expert_count), 0)
    expert_ids = lax.broadcasted_iota(jnp.int32, (expert_count, expert_count), 1)
    table = jnp.where(device_ids == own_expert, counts[None, :], 0)
    table = lax.psum(table.reshape(-1, LANES), EXPERT).reshape(expert_count, expert_count)
    arrived = jnp.sum(jnp.where(expert_ids == own_expert, table, 0), axis=1)
    plane_ids = lax.broadcasted_iota(jnp.int32, (dp_count, LANES), 0)
    lane_ids = lax.broadcasted_iota(jnp.int32, (dp_count, LANES), 1)
    plane_row = jnp.pad(jnp.sum(table, axis=0).astype(jnp.float32), (0, LANES - expert_count))
    both = jnp.concatenate(
        [
            jnp.where(plane_ids == own_dp, plane_row[None, :], 0.0),
            jnp.where(plane_ids == own_dp, gate_weights.reshape(-1, LANES), 0.0),
        ]
    )
    both = lax.psum(both, "dp")
    plane_counts = both[:dp_count].astype(jnp.int32)
    most_rows = jnp.max(plane_counts)
    earlier = jnp.logical_and(plane_ids < own_dp, lane_ids == own_expert)
    first_slot = jnp.sum(jnp.where(earlier, plane_counts, 0))
    gates_all = jnp.concatenate([both[dp_count:].reshape(-1), jnp.zeros((rows_all,), jnp.float32)])
    within = lax.broadcasted_iota(jnp.int32, (expert_count, MOST), 1)
    target = jnp.where(within < arrived[:, None], exclusive(arrived)[:, None] + within, -1).reshape(
        rows_all
    )

    def experts(rows, plane_rows):
        slot_ids = lax.broadcasted_iota(jnp.int32, (rows_all, plane_rows), 1)
        place_table = (target[:, None] == slot_ids).astype(jnp.bfloat16)
        plane = lax.dot_general(
            place_table, rows, (((0,), (0,)), ((), ())), preferred_element_type=jnp.float32
        ).astype(jnp.bfloat16)
        slot_rows = lax.all_gather(plane, "dp", axis=0, tiled=True)
        hidden = jnp.maximum(
            jnp.dot(slot_rows, weight_in[0], preferred_element_type=jnp.float32), 0.0
        ).astype(jnp.bfloat16)
        share = jnp.dot(hidden, weight_out[0], preferred_element_type=jnp.float32)
        out = lax.psum_scatter(
            share.astype(jnp.bfloat16), "dp", scatter_dimension=0, tiled=True
        ).astype(jnp.float32)
        gates = lax.dynamic_slice_in_dim(gates_all, first_slot, plane_rows, 0)
        scaled = (gates[:, None] * out).astype(jnp.bfloat16)
        returned = jnp.dot(place_table, scaled, preferred_element_type=jnp.float32)
        return returned.astype(jnp.bfloat16)

    fair = slots_dp + slots_dp // 4
    sent_back = lax.cond(
        most_rows <= fair,
        lambda rows: experts(rows, fair),
        lambda rows: experts(rows, rows_all),
        arrived_rows,
    )
    results = lax.all_to_all(
        sent_back.reshape(expert_count, MOST, width),
        EXPERT,
        split_axis=0,
        concat_axis=0,
        tiled=True,
    ).reshape(rows_all, width)
    combined = lax.dot_general(
        pack_table, results, (((0,), (0,)), ((), ())), preferred_element_type=jnp.float32
    )
    return combined.astype(jnp.bfloat16)


def solution(mesh):
    split = Mesh(
        mesh.devices.reshape(mesh.shape["dp"], 4, 4, 2), ("dp", "expert_0", "expert_1", "expert_2")
    )
    placed = (
        P(DP_EXPERT, None),
        P(None, DP_EXPERT),
        P(),
        P(EXPERT, None, "dp"),
        P(EXPERT, "dp", None),
        P(EXPERT, "dp"),
    )
    return jax.shard_map(
        on_device, mesh=split, in_specs=placed, out_specs=P(DP_EXPERT, None), check_vma=False
    )
```

profile of v0, /device:TPU:1, one launch (start us, length us, event | category | flops | bytes accessed | tf_op | source)
XLA Modules:
  0.0 348.8 jit_solution(17893966849262882347)
XLA Ops:
  6.5 0.9 convert_bitcast_fusion.1
  7.5 0.6 reduce-window.18
  8.1 0.2 slice_reduce_fusion
  8.3 0.1 iota.90
  8.4 0.1 convert_subtract_fusion
  8.5 1.5 fusion.19
  10.0 8.6 %all-to-all-start = ((bf16[32,8,2048]{2,1,0:T(8,128)(2,1)}), bf16[32,8,2048]{2,1,0:T(8,128)(2,1)S(1)}, u32[]{:S(2)}, u32[]{:S(2)}) async-start(bf16[32,8,2048]{2,1,0:T(8,128)(2,1)} %fusion.19), calls=%async_computation.2 | async-start | bytes 2097152 | tf_op jit(solution)/shard_map/all_to_all | solution.py:33
  18.7 0.1 iota.80
  18.9 127.0 %psum.14 = s32[32,32]{1,0:T(8,128)S(1)} all-reduce(s32[32,32]{1,0:T(8,128)S(1)} %reshape.73), channel_id=1, replica_groups=mesh['dp'=8,'expert_0'=4,'expert_1'=4,'expert_2'=2] {'expert_0','expert_..., use_global_device_ids=true, to_apply=%region_3.4 | all-reduce | flops 1024 | bytes 8192 | tf_op jit(solution)/shard_map/psum | solution.py:39
  145.9 0.1 select_reduce_fusion
  146.1 16.5 %psum.15 = f32[16,128]{1,0:T(8,128)S(1)} all-reduce(f32[16,128]{1,0:T(8,128)S(1)} %pad_maximum_fusion), channel_id=1, replica_groups=mesh['dp'=8,'expert_0'=4,'expert_1'=4,'expert_2'=2] {'dp'}, use_global_device_ids=true, to_apply=%region_5.6 | all-reduce | flops 2048 | bytes 16384 | tf_op jit(solution)/shard_map/psum | solution.py:50
  162.7 0.8 select_reduce_fusion.1
  164.2 0.1 copy.19
  164.3 0.1 reduce.1
  164.5 151.7 %conditional.2 = (bf16[256,2048]{1,0:T(8,128)(2,1)S(1)}) conditional(s32[]{:T(128)} %convert_element_type.61, (s32[32,8]{1,0:T(8,128)S(1)}, s32[]{:T(128)}, f32[1280]{0:T(1024)S(1)}, bf16[256,2048]{1,0:T(8,128)(2,1)S(1)}, bf16[1,2048,1024]{2,1,0:T(8,128)(2,1)}, /*index=5*/bf16[1,1024,2048]{2,1,0:T(8,128)(2,1)}) %tuple.30, (s32[32,8]{1,0:T(8,128)S(1)}, ...), branch_computations={%region_10.12_spmd, %region_12.14_spmd} | conditional | flops 17727356928 | bytes 85990520
  164.6 0.1 eq.49
  164.7 1.3 convolution_convert_fusion.3
  166.0 0.2 reduce-scatter.5.cloned.1.call-start
  166.2 67.1 %all-gather.5.cloned.1.call-done = bf16[1280,2048]{1,0:T(8,128)(2,1)} async-done(((bf16[160,2048]{1,0:T(8,128)(2,1)}), bf16[1280,2048]{1,0:T(8,128)(2,1)}) %all-gather.5.cloned.1.call-update) | async-done | bytes 5242896 | tf_op jit(solution)/shard_map/cond/branch_1_fun/all_gather | solution.py:67
  233.4 16.9 %convolution_convert_fusion.2 = bf16[1280,2048]{1,0:T(8,128)(2,1)} fusion(bf16[1,1024,2048]{2,1,0:T(8,128)(2,1)} %get-tuple-element.45, bf16[1280,2048]{1,0:T(8,128)(2,1)} %all-gather.5.cloned.1.call-done, bf16[1,2048,1024]{2,1,0:T(8,128)(2,1)} %get-tuple-element.44), kind=kOutput, calls=%fused_computation.13 | convolution fusion | flops 10742661120 | bytes 18874368 | tf_op jit(solution)/shard_map/cond/branch_1_fun/dot_general | solution.py:71
  252.0 62.3 %reduce-scatter.5.cloned.1.call-done = bf16[160,2048]{1,0:T(8,128)(2,1)} async-done(((bf16[1280,2048]{1,0:T(8,128)(2,1)}), bf16[160,2048]{1,0:T(8,128)(2,1)}) %reduce-scatter.5.cloned.1.call-update) | async-done | bytes 655376 | tf_op jit(solution)/shard_map/cond/branch_1_fun/reduce_scatter | solution.py:72
  314.4 1.6 fusion.13
  316.2 24.3 %all_to_all.10 = bf16[32,8,2048]{2,1,0:T(8,128)(2,1)S(1)} all-to-all(bf16[32,8,2048]{2,1,0:T(8,128)(2,1)S(1)} %bitcast.57), channel_id=1, replica_groups=mesh['dp'=8,'expert_0'=4,'expert_1'=4,'expert_2'=2] {'expert_0','expert_..., dimensions={0} | all-to-all | bytes 2097152 | tf_op jit(solution)/shard_map/all_to_all | solution.py:87
  340.5 1.5 fusion.18
  (32 shorter events, 0.7 us)
Async XLA Ops:
  6.5 2.0 copy-start
  6.5 139.5 %copy-start.1 = (f32[1,128]{1,0:T(1,128)S(1)}, f32[1,128]{1,0:T(1,128)}, u32[]{:S(2)}) copy-start(f32[1,128]{1,0:T(1,128)} %param.13) | copy-start | bytes 1540
  10.0 154.5 %all-to-all-start = ((bf16[32,8,2048]{2,1,0:T(8,128)(2,1)}), bf16[32,8,2048]{2,1,0:T(8,128)(2,1)S(1)}, u32[]{:S(2)}, u32[]{:S(2)}) async-start(bf16[32,8,2048]{2,1,0:T(8,128)(2,1)} %fusion.19), calls=%async_computation.2 | async-start | bytes 2097152 | tf_op jit(solution)/shard_map/all_to_all | solution.py:33
  164.5 68.8 %all-gather.5.cloned.1.call-start = ((), (), s32[]{:S(2)}) async-start(), calls=%async_computation.6 | async-start | bytes 5898240 | tf_op jit(solution)/shard_map/cond/branch_1_fun/all_gather | solution.py:67
  166.0 148.4 %reduce-scatter.5.cloned.1.call-start = ((), (), s32[]{:S(2)}) async-start(), calls=%async_computation.7 | async-start | bytes 5898240 | tf_op jit(solution)/shard_map/cond/branch_1_fun/reduce_scatter | solution.py:72
Sparse Core Ops, SparseCore 0:
  167.1 66.1 all-gather.4
  250.4 63.9 reduce-scatter.4
where the time goes:
time: 349 us
  blocking collectives  168 us (48%)
  waiting for transfers between devices  129 us (37%)
  matrix products  22.7 us (7%)
  between operations  14.2 us (4%)
  starting transfers between devices  8.84 us (3%)
    psum x1, blocking collectives, on_device(): lax.psum(table.reshape(-1, LANES), EXPERT)  127 us
    all_gather x1, waiting for transfers between devices, experts(): slot_rows = lax.all_gather(plane, 'dp', axis=0, tiled=True)  67.1 us
    reduce_scatter x1, waiting for transfers between devices, experts(): lax.psum_scatter(share.astype(jnp.bfloat16), 'dp', scatter_dimension=0, t...  62.3 us
    all_to_all x1, blocking collectives, on_device(): lax.all_to_all(sent_back.reshape(expert_count, MOST, width), EXPERT, spli...  24.3 us
    dot_general x1, matrix products, experts(): share = jnp.dot(hidden, weight_out[0], preferred_element_type=jnp.float32)  16.9 us
    psum x1, blocking collectives, on_device(): both = lax.psum(both, 'dp')  16.5 us
    all_to_all x1, starting transfers between devices, on_device(): lax.all_to_all(packed.reshape(expert_count, MOST, width), EXPERT, split_a...  8.58 us
  transfers between devices with their start and end apart: 3, of which 2 were waited for; matrix products, arithmetic and copies ran while one was open for 1% of the time, Pallas kernels for 0%

commit v1 on v0

--- a/solution.py
+++ b/solution.py
@@ -36,7 +36,9 @@
     device_ids = lax.broadcasted_iota(jnp.int32, (expert_count, expert_count), 0)
     expert_ids = lax.broadcasted_iota(jnp.int32, (expert_count, expert_count), 1)
     table = jnp.where(device_ids == own_expert, counts[None, :], 0)
-    table = lax.psum(table.reshape(-1, LANES), EXPERT).reshape(expert_count, expert_count)
+    table = lax.psum(
+        lax.psum(table.reshape(-1, LANES), "expert_0"), ("expert_1", "expert_2")
+    ).reshape(expert_count, expert_count)
     arrived = jnp.sum(jnp.where(expert_ids == own_expert, table, 0), axis=1)
     plane_ids = lax.broadcasted_iota(jnp.int32, (dp_count, LANES), 0)
     lane_ids = lax.broadcasted_iota(jnp.int32, (dp_count, LANES), 1)

time: 349 us -> 260 us (0.74)
  blocking collectives: 168 us -> 80.1 us
    psum x1 -> x2, blocking collectives: 127 us -> 39.3 us  [the longest x1 22.7 us: on_device(): lax.psum(lax.psum(table.reshape(-1, LANES), 'expert_0'), ('expert_1', 'ex...]
where the time goes in v1:
time: 260 us; the launch traced here: 259 us
  waiting for transfers between devices  128 us (49%)
  blocking collectives  80.1 us (31%)
  matrix products  22.7 us (9%)
  between operations  14.2 us (5%)
  starting transfers between devices  8.84 us (3%)
  other arithmetic  2.95 us (1%)
    all_gather x1, waiting for transfers between devices, experts(): slot_rows = lax.all_gather(plane, 'dp', axis=0, tiled=True)  65.2 us
    reduce_scatter x1, waiting for transfers between devices, experts(): lax.psum_scatter(share.astype(jnp.bfloat16), 'dp', scatter_dimension=0, t...  62.3 us
    all_to_all x1, blocking collectives, on_device(): lax.all_to_all(sent_back.reshape(expert_count, MOST, width), EXPERT, spli...  24.3 us
    psum x1, blocking collectives, on_device(): lax.psum(lax.psum(table.reshape(-1, LANES), 'expert_0'), ('expert_1', 'ex...  22.7 us
    dot_general x1, matrix products, experts(): share = jnp.dot(hidden, weight_out[0], preferred_element_type=jnp.float32)  16.9 us
    psum x1, blocking collectives, on_device(): lax.psum(table.reshape(-1, LANES), 'expert_0')  16.6 us
    psum x1, blocking collectives, on_device(): both = lax.psum(both, 'dp')  16.5 us
    all_to_all x1, starting transfers between devices, on_device(): lax.all_to_all(packed.reshape(expert_count, MOST, width), EXPERT, split_a...  8.58 us
  transfers between devices with their start and end apart: 3, of which 2 were waited for; matrix products, arithmetic and copies ran while one was open for 1% of the time, Pallas kernels for 0%

profile of v1, /device:TPU:1, one launch (start us, length us, event | category | flops | bytes accessed | tf_op | source)
XLA Modules:
  0.0 259.2 jit_solution(16805566919057546236)
XLA Ops:
  6.5 0.9 convert_bitcast_fusion.1
  7.5 0.6 reduce-window.18
  8.1 0.2 slice_reduce_fusion
  8.3 0.1 iota.90
  8.4 0.1 convert_subtract_fusion
  8.5 1.5 fusion.19
  10.0 8.6 %all-to-all-start = ((bf16[32,8,2048]{2,1,0:T(8,128)(2,1)}), bf16[32,8,2048]{2,1,0:T(8,128)(2,1)S(1)}, u32[]{:S(2)}, u32[]{:S(2)}) async-start(bf16[32,8,2048]{2,1,0:T(8,128)(2,1)} %fusion.19), calls=%async_computation.2 | async-start | bytes 2097152 | tf_op jit(solution)/shard_map/all_to_all | solution.py:33
  18.7 0.1 iota.80
  18.9 16.6 %psum.21 = s32[8,128]{1,0:T(8,128)S(1)} all-reduce(s32[8,128]{1,0:T(8,128)S(1)} %broadcast_select_fusion.2), channel_id=1, replica_groups=mesh['dp'=8,'expert_0'=4,'expert_1'=4,'expert_2'=2] {'expert_0'}, use_global_device_ids=true, to_apply=%region_3.4 | all-reduce | flops 1024 | bytes 8192 | tf_op jit(solution)/shard_map/psum | solution.py:40
  35.5 22.7 %psum.22 = s32[32,32]{1,0:T(8,128)S(1)} all-reduce(s32[32,32]{1,0:T(8,128)S(1)} %reshape.73), channel_id=1, replica_groups=mesh['dp'=8,'expert_0'=4,'expert_1'=4,'expert_2'=2] {'expert_1','expert_2'}, use_global_device_ids=true, to_apply=%region_4.5 | all-reduce | flops 1024 | bytes 8192 | tf_op jit(solution)/shard_map/psum | solution.py:39
  58.2 0.1 select_reduce_fusion
  58.5 16.5 %psum.23 = f32[16,128]{1,0:T(8,128)S(1)} all-reduce(f32[16,128]{1,0:T(8,128)S(1)} %pad_maximum_fusion), channel_id=1, replica_groups=mesh['dp'=8,'expert_0'=4,'expert_1'=4,'expert_2'=2] {'dp'}, use_global_device_ids=true, to_apply=%region_6.7 | all-reduce | flops 2048 | bytes 16384 | tf_op jit(solution)/shard_map/psum | solution.py:52
  75.0 0.8 select_reduce_fusion.1
  76.5 0.1 copy.19
  76.6 0.1 reduce.1
  76.8 149.8 %conditional.2 = (bf16[256,2048]{1,0:T(8,128)(2,1)S(1)}) conditional(s32[]{:T(128)} %convert_element_type.61, (s32[32,8]{1,0:T(8,128)S(1)}, s32[]{:T(128)}, f32[1280]{0:T(1024)S(1)}, bf16[256,2048]{1,0:T(8,128)(2,1)S(1)}, bf16[1,2048,1024]{2,1,0:T(8,128)(2,1)}, /*index=5*/bf16[1,1024,2048]{2,1,0:T(8,128)(2,1)}) %tuple.30, (s32[32,8]{1,0:T(8,128)S(1)}, ...), branch_computations={%region_11.13_spmd, %region_13.15_spmd} | conditional | flops 17727356928 | bytes 85990520
  77.0 1.3 convolution_convert_fusion.3
  78.3 0.2 reduce-scatter.5.cloned.1.call-start
  78.5 65.2 %all-gather.5.cloned.1.call-done = bf16[1280,2048]{1,0:T(8,128)(2,1)} async-done(((bf16[160,2048]{1,0:T(8,128)(2,1)}), bf16[1280,2048]{1,0:T(8,128)(2,1)}) %all-gather.5.cloned.1.call-update) | async-done | bytes 5242896 | tf_op jit(solution)/shard_map/cond/branch_1_fun/all_gather | solution.py:69
  143.8 16.9 %convolution_convert_fusion.2 = bf16[1280,2048]{1,0:T(8,128)(2,1)} fusion(bf16[1,1024,2048]{2,1,0:T(8,128)(2,1)} %get-tuple-element.45, bf16[1280,2048]{1,0:T(8,128)(2,1)} %all-gather.5.cloned.1.call-done, bf16[1,2048,1024]{2,1,0:T(8,128)(2,1)} %get-tuple-element.44), kind=kOutput, calls=%fused_computation.13 | convolution fusion | flops 10742661120 | bytes 18874368 | tf_op jit(solution)/shard_map/cond/branch_1_fun/dot_general | solution.py:73
  162.4 62.3 %reduce-scatter.5.cloned.1.call-done = bf16[160,2048]{1,0:T(8,128)(2,1)} async-done(((bf16[1280,2048]{1,0:T(8,128)(2,1)}), bf16[160,2048]{1,0:T(8,128)(2,1)}) %reduce-scatter.5.cloned.1.call-update) | async-done | bytes 655376 | tf_op jit(solution)/shard_map/cond/branch_1_fun/reduce_scatter | solution.py:74
  224.8 1.6 fusion.13
  226.6 24.3 %all_to_all.10 = bf16[32,8,2048]{2,1,0:T(8,128)(2,1)S(1)} all-to-all(bf16[32,8,2048]{2,1,0:T(8,128)(2,1)S(1)} %bitcast.57), channel_id=1, replica_groups=mesh['dp'=8,'expert_0'=4,'expert_1'=4,'expert_2'=2] {'expert_0','expert_..., dimensions={0} | all-to-all | bytes 2097152 | tf_op jit(solution)/shard_map/all_to_all | solution.py:89
  250.9 1.5 fusion.18
  (33 shorter events, 0.8 us)
Async XLA Ops:
  6.5 2.0 copy-start
  6.5 51.8 %copy-start.1 = (f32[1,128]{1,0:T(1,128)S(1)}, f32[1,128]{1,0:T(1,128)}, u32[]{:S(2)}) copy-start(f32[1,128]{1,0:T(1,128)} %param.13) | copy-start | bytes 1540
  10.0 66.9 %all-to-all-start = ((bf16[32,8,2048]{2,1,0:T(8,128)(2,1)}), bf16[32,8,2048]{2,1,0:T(8,128)(2,1)S(1)}, u32[]{:S(2)}, u32[]{:S(2)}) async-start(bf16[32,8,2048]{2,1,0:T(8,128)(2,1)} %fusion.19), calls=%async_computation.2 | async-start | bytes 2097152 | tf_op jit(solution)/shard_map/all_to_all | solution.py:33
  76.9 66.9 %all-gather.5.cloned.1.call-start = ((), (), s32[]{:S(2)}) async-start(), calls=%async_computation.6 | async-start | bytes 5898240 | tf_op jit(solution)/shard_map/cond/branch_1_fun/all_gather | solution.py:69
  78.3 146.5 %reduce-scatter.5.cloned.1.call-start = ((), (), s32[]{:S(2)}) async-start(), calls=%async_computation.7 | async-start | bytes 5898240 | tf_op jit(solution)/shard_map/cond/branch_1_fun/reduce_scatter | solution.py:74
Sparse Core Ops, SparseCore 0:
  79.5 64.2 all-gather.4
  160.8 63.9 reduce-scatter.4
